TPU v7x, 256 devices: a whole 4x4x8 slice. The times are simulated.
256 devices in a mesh: feat: 8 (over y, core), rows: 32 (over z, x).
Axes of the slice: x: 4, y: 4, z: 8, core: 2. Of those that a mesh axis runs over, the one named last changes fastest.
Arguments:
- test_cells: float32 [256, 96, 192], P('rows', 'feat'), may hold values from -12 to 12
- train_cells: float32 [16384, 96, 192], P('rows', 'feat'), may hold values from -6 to 6
- w_query: float32 [192, 192], P('feat'), may hold values from -1.5 to 1.5
- w_key: float32 [192, 192], P('feat'), may hold values from -1.5 to 1.5
- w_value: float32 [192, 192], P('feat'), may hold values from -0.4375 to 0.4375
- w_out: float32 [192, 192], P('feat'), may hold values from -0.4375 to 0.4375
Outputs:
- attended: float32 [256, 96, 192], P('rows', 'feat')
All inputs are finite; a program needn't handle non-finite values.
Results may differ from a plain program's by a relative error of at most 0.0003.
Values sent between devices are 32-bit elements; how exact they have to be, the bound alone decides.
A program may use at most 64 MiB of HBM per device.

v0:
```python
import jax
import jax.numpy as jnp
from jax import lax
from jax.sharding import Mesh
from jax.sharding import PartitionSpec as P

HEADS = 6
HEAD = 32
ROWS = ("rows_0", "rows_1")


def in_one_piece(arrays, axis, dim, along):
    widths = [a.shape[along] for a in arrays]
    both = jnp.concatenate(arrays, axis=along)
    out = lax.all_gather(both, axis, axis=dim, tiled=True)
    return tuple(jnp.split(out, [sum(widths[:k]) for k in range(1, len(widths))], axis=along))


def whole_of(x, axes, dim):
    out = x
    for number in range(len(axes) - 1, -1, -1):
        out = lax.all_gather(out, axes[number], axis=dim, tiled=True)
    return out


def sent_to_all(x, axis):
    copies = jnp.broadcast_to(x, (lax.axis_size(axis), *x.shape))
    return lax.all_to_all(copies, axis, split_axis=0, concat_axis=0, tiled=True)


def of_everyone(x, axis):
    everything = sent_to_all(x, axis)
    return jnp.max(everything, axis=0)


def in_blocks(x, dim, count):
    lengths = x.shape
    parts = x.reshape(*lengths[:dim], count, lengths[dim] // count, *lengths[dim + 1 :])
    return jnp.moveaxis(parts, dim, 0)


def sent_and_summed(x, axis, dim):
    parts = in_blocks(x, dim, lax.axis_size(axis))
    arrived = lax.all_to_all(parts, axis, split_axis=0, concat_axis=0, tiled=True)
    return arrived.sum(axis=0)


def in_one_piece_2(arrays, axis, dim, along):
    both = jnp.concatenate(arrays, axis=along)
    out, at, gathered = (sent_and_summed(both, axis, dim), 0, [])
    for a in arrays:
        gathered.append(lax.slice_in_dim(out, at, at + a.shape[along], axis=along))
        at += a.shape[along]
    return tuple(gathered)


def rescale(weighted, factor):
    shape = weighted.shape
    split = weighted.reshape(shape[0], shape[1], factor.shape[2], shape[2] // factor.shape[2])
    return (split * factor[:, :, :, None]).reshape(shape)


def per_device(test_cells, train_cells, w_query, w_key, w_value, w_out):
    highest = lax.Precision.HIGHEST
    full_query, full_key, full_value, full_out = in_one_piece(
        (w_query, w_key, w_value, w_out), "feat", 0, 1
    )
    local_queries = jnp.einsum("rfd,de->rfe", test_cells, full_query, precision=highest) * HEAD ** (
        -0.5
    )
    queries = whole_of(local_queries, ROWS, 0)
    key_rows = jnp.einsum("rfd,de->rfe", train_cells, full_key, precision=highest)
    value_rows = jnp.einsum("rfd,de->rfe", train_cells, full_value, precision=highest)
    test_rows = queries.shape[0]
    train_rows = key_rows.shape[0]
    width = queries.shape[2]
    head_count = HEADS
    head_size = width // head_count

    def one_feature(feature):
        query_part = lax.dynamic_index_in_dim(queries, feature, 1, keepdims=False).reshape(
            test_rows, head_count, head_size
        )
        key_part = lax.dynamic_index_in_dim(key_rows, feature, 1, keepdims=False).reshape(
            train_rows, head_count, head_size
        )
        value_part = lax.dynamic_index_in_dim(value_rows, feature, 1, keepdims=False).reshape(
            train_rows, head_count, head_size
        )
        scores = jnp.einsum("qhe,khe->hqk", query_part, key_part, precision=highest)
        maxima = jnp.max(scores, axis=-1, keepdims=True)
        probs = jnp.exp(scores - maxima)
        totals = jnp.sum(probs, axis=-1)
        weighted = jnp.einsum("hqk,khe->qhe", probs, value_part, precision=highest)
        return (
            jnp.transpose(maxima[:, :, 0]),
            jnp.transpose(totals),
            weighted.reshape(test_rows, width),
        )

    features = train_cells.shape[1]
    maxima, totals, weighted = lax.map(one_feature, jnp.arange(features, dtype=jnp.int32))
    top = of_everyone(maxima, ROWS)
    factor = jnp.exp(maxima - top)
    weighted, totals = in_one_piece_2((rescale(weighted, factor), totals * factor), ROWS, 1, 2)
    mixed = rescale(weighted, 1.0 / totals)
    return jnp.einsum("ftd,de->tfe", mixed, full_out, precision=highest)


def solution(mesh):
    finer = Mesh(mesh.devices.reshape(mesh.shape["feat"], 8, 4), ("feat", "rows_0", "rows_1"))
    return jax.shard_map(
        per_device,
        mesh=finer,
        in_specs=(
            P(ROWS, "feat", None),
            P(ROWS, "feat", None),
            P("feat", None),
            P("feat", None),
            P("feat", None),
            P("feat", None),
        ),
        out_specs=P(ROWS, "feat", None),
        check_vma=False,
    )
```

profile of v0, /device:TPU:2, one launch (start us, length us, event | category | flops | bytes accessed | tf_op | source)
XLA Modules:
  0.0 407.3 jit_solution(1469674603430756197)
XLA Ops:
  7.4 13.7 %all_gather.9 = f32[192,768]{1,0:T(8,128)S(1)} all-gather(f32[24,768]{1,0:T(8,128)S(1)} %pad_maximum_fusion), channel_id=1, replica_groups=mesh['feat'=8,'rows_0'=8,'rows_1'=4] {'feat'}, dimensions={0}, use_global_device_ids=true | all-gather | bytes 663552 | tf_op jit(solution)/shard_map/all_gather | solution.py:15
  21.5 13.3 %all_gather.10 = f32[32,12,192]{2,0,1:T(8,128)} all-gather(f32[8,12,192]{2,0,1:T(8,128)S(1)} %copy.33), channel_id=1, replica_groups=mesh['feat'=8,'rows_0'=8,'rows_1'=4] {'rows_1'}, dimensions={0}, use_global_device_ids=true | all-gather | bytes 368640 | tf_op jit(solution)/shard_map/all_gather | solution.py:22
  34.9 9.0 %convolution_bitcast_fusion.1 = f32[512,12,192]{0,2,1:T(8,128)} fusion(f32[512,12,192]{0,2,1:T(8,128)} %param.9, f32[192,768]{1,0:T(8,128)S(1)} %all_gather.9), kind=kOutput, calls=%fused_computation.13 | convolution fusion | flops 2717908992 | bytes 9633792 | tf_op jit(solution)/shard_map/rfd,de->rfe/dot_general | solution.py:72
  43.9 6.1 %convolution_bitcast_fusion = f32[512,12,192]{0,2,1:T(8,128)} fusion(f32[512,12,192]{0,2,1:T(8,128)S(1)} %bitcast.69, f32[192,768]{1,0:T(8,128)S(1)} %all_gather.9), kind=kOutput, calls=%fused_computation.12 | convolution fusion | flops 2717908992 | bytes 9633792 | tf_op jit(solution)/shard_map/rfd,de->rfe/dot_general | solution.py:73
  49.9 32.0 %all-gather.2.cloned.1.call-done = f32[256,12,192]{2,0,1:T(8,128)} async-done(((f32[32,12,192]{2,0,1:T(8,128)}), f32[256,12,192]{2,0,1:T(8,128)}) %all-gather.2.cloned.1.call-update) | async-done | bytes 2359312 | tf_op jit(solution)/shard_map/all_gather | solution.py:22
  84.4 146.3 %while.14 = (s32[]{:T(128)}, f32[12,256,6]{1,2,0:T(8,128)S(1)}, f32[12,256,6]{1,2,0:T(8,128)S(1)}, f32[12,256,192]{1,2,0:T(8,128)}, s32[12]{0:T(128)S(1)}, /*ind...) while((s32[]{:T(128)}, f32[12,256,6]{1,2,0:T(8,128)S(1)}, ...), condition=%wide.region_3.4_spmd, body=%wide.region_0.3_spmd.sunk | while | flops 607122432 | bytes 13033655 | solution.py:102
  92.8 3.1 fusion.24
  105.0 3.1 fusion.24
  117.1 3.1 fusion.24
  124.6 2.8 fusion.22
  129.4 3.1 fusion.24
  141.6 3.1 fusion.24
  153.8 3.1 fusion.24
  165.9 3.1 fusion.24
  178.1 3.1 fusion.24
  190.3 3.1 fusion.24
  197.7 2.8 fusion.22
  202.5 3.1 fusion.24
  214.7 3.1 fusion.24
  222.1 2.8 fusion.22
  226.9 3.1 fusion.24
  231.0 80.0 %all_to_all.10 = f32[32,12,256,6]{2,3,1,0:T(8,128)S(1)} all-to-all(f32[32,12,256,6]{2,3,1,0:T(8,128)S(1)} %broadcast_in_dim.21), channel_id=1, replica_groups=mesh['feat'=8,'rows_0'=8,'rows_1'=4] {'rows_0','rows_1'}, dimensions={0} | all-to-all | bytes 4718592 | tf_op jit(solution)/shard_map/all_to_all | solution.py:28
  312.9 3.3 bitcast_multiply_fusion
  320.8 77.1 %all_to_all.11 = f32[32,12,8,198]{3,2,1,0:T(8,128)S(1)} all-to-all(f32[32,12,8,198]{3,2,1,0:T(8,128)S(1)} %copy.39), channel_id=1, replica_groups=mesh['feat'=8,'rows_0'=8,'rows_1'=4] {'rows_0','rows_1'}, dimensions={0} | all-to-all | bytes 4866048 | tf_op jit(solution)/shard_map/all_to_all | solution.py:44
  (126 shorter events, 90.5 us)
Async XLA Ops:
  6.5 14.6 %copy-start = (f32[8,12,192]{2,0,1:T(8,128)S(1)}, f32[8,12,192]{2,0,1:T(8,128)}, u32[]{:S(2)}) copy-start(f32[8,12,192]{2,0,1:T(8,128)} %param.8) | copy-start | bytes 221188
  6.5 75.5 %all-gather.2.cloned.1.call-start = ((), (), s32[]{:S(2)}) async-start(), calls=%async_computation.2 | async-start | bytes 3538944 | tf_op jit(solution)/shard_map/all_gather | solution.py:22
  21.2 22.7 %copy-start.1 = (f32[192,768]{1,0:T(8,128)}, f32[192,768]{1,0:T(8,128)S(1)}, u32[]{:S(2)}) copy-start(f32[192,768]{1,0:T(8,128)S(1)} %all_gather.9) | copy-start | bytes 1769476
  34.9 9.0 %slice-start = ((s8[4718592]{0:T(1024)(128)(4,1)}), s8[524288]{0:T(1024)(128)(4,1)S(1)}, s32[]{:S(2)}) async-start(s8[4718592]{0:T(1024)(128)(4,1)} %bitcast.68), calls=%async_computation.3 | async-start | bytes 1048576
  34.9 9.0 %slice-start.1 = ((s8[4718592]{0:T(1024)(128)(4,1)}), s8[4194304]{0:T(1024)(128)(4,1)S(1)}, s32[]{:S(2)}) async-start(s8[4718592]{0:T(1024)(128)(4,1)} %bitcast.68), calls=%async_computation.4 | async-start | bytes 8388608
Sparse Core Ops, SparseCore 0:
  35.0 46.9 all-gather.1
where the time goes:
time: 409 us; the launch traced here: 407 us
  blocking collectives  184 us (45%)
  matrix products  87.3 us (21%)
  local copies, waits for them, and re-layouts  49.2 us (12%)
  waiting for transfers between devices  32.1 us (8%)
  loops' own time  23.3 us (6%)
  other arithmetic  17.8 us (4%)
  between operations  13.6 us (3%)
    all_to_all x1, blocking collectives, sent_to_all(): return lax.all_to_all(copies, axis, split_axis=0, concat_axis=0, tiled=True)  80 us
    all_to_all x1, blocking collectives, sent_and_summed(): lax.all_to_all(parts, axis, split_axis=0, concat_axis=0, tiled=True)  77.1 us
    dot_general x12, matrix products, one_feature(): weighted = jnp.einsum('hqk,khe->qhe', probs, value_part, precision=highest)  37.1 us
    dot_general x12, matrix products, one_feature(): scores = jnp.einsum('qhe,khe->hqk', query_part, key_part, precision=highest)  33.7 us
    all_gather x1, waiting for transfers between devices, whole_of(): out = lax.all_gather(out, axes[number], axis=dim, tiled=True)  32 us
    another operation x1, loops' own time, per_device(): lax.map(one_feature, jnp.arange(features, dtype=jnp.int32))  23.3 us
    all_gather x1, blocking collectives, in_one_piece(): out = lax.all_gather(both, axis, axis=dim, tiled=True)  13.7 us
    all_gather x1, blocking collectives, whole_of(): out = lax.all_gather(out, axes[number], axis=dim, tiled=True)  13.3 us
  transfers between devices with their start and end apart: 1, of which 1 were waited for; matrix products, arithmetic and copies ran while one was open for 4% of the time, Pallas kernels for 0%

commit v1 on v0

v1 whole, which is shorter than its diff:
```python
import functools

import jax
import jax.numpy as jnp
from jax import lax
from jax.experimental import pallas as pl
from jax.experimental.pallas import tpu as pltpu
from jax.sharding import PartitionSpec as P

BF = jnp.bfloat16
F32 = jnp.float32
HEADS = 6
HEAD = 32
LOG2E = 1.4426950408889634
NZ, NX, NF = 8, 4, 8
VROWS = 2 * HEAD + 16
GROUP = 3
WIDE = 640
MESH = pl.DeviceIdType.MESH


def split(x):
    hi = x.astype(BF)
    return hi, (x - hi.astype(F32)).astype(BF)


def tree(n1, n2):
    low1, high1 = -(n1 // 2), n1 // 2 - 1
    events = []
    for i in range(low1, high1 + 1):
        reach_right, reach_left = (n2 // 2, n2 // 2 - 1) if i % 2 == 0 else (n2 // 2 - 1, n2 // 2)
        for j in range(-reach_right, reach_left + 1):
            children = []
            if j == 0:
                if i <= 0 and i > low1:
                    children.append((0, 1, i - 1, 0))
                if i >= 0 and i < high1:
                    children.append((0, -1, i + 1, 0))
            if j <= 0 and j > -reach_right:
                children.append((1, 1, i, j - 1))
            if j >= 0 and j < reach_left:
                children.append((1, -1, i, j + 1))
            events.append((abs(i) + abs(j), i, j, children))
    return sorted(events)


def kernel(
    x_hbm, t_ref, wq_ref, wk_ref, wv_ref, wo_ref, out_ref,
    xb, wb, gat, kp, vp, qp, wkv, wqc, woc, ot, own, zr, zl, xr, xl,
    x_sem, w_send, w_recv, g_send, g_recv, r_send, r_recv,
):
    width = HEADS * HEAD
    features = x_hbm.shape[0]
    rows = x_hbm.shape[2]
    tests = gat.shape[1] * gat.shape[2]
    feat, place = lax.axis_index("feat"), lax.axis_index("rows")
    z, x = place // NX, place % NX

    def at(dz, dx):
        return lax.rem(z + dz + NZ, NZ) * NX + lax.rem(x + dx + NX, NX)

    for f in range(features):
        pltpu.make_async_copy(x_hbm.at[f], xb.at[f], x_sem.at[f]).start()

    wb[feat] = jnp.concatenate([wk_ref[...], wv_ref[...], wq_ref[...], wo_ref[...]], axis=1)
    for p in range(features // 2):
        gat[p, place] = jnp.concatenate([t_ref[2 * p], t_ref[2 * p + 1]], axis=1)

    barrier = pltpu.get_barrier_semaphore()
    for dz, dx in ((1, 0), (-1, 0), (0, 1), (0, -1)):
        pl.semaphore_signal(
            barrier, inc=1, device_id={"feat": feat, "rows": at(dz, dx)}, device_id_type=MESH
        )
    for k in range(1, NF):
        pl.semaphore_signal(
            barrier,
            inc=1,
            device_id={"feat": lax.rem(feat + k, NF), "rows": place},
            device_id_type=MESH,
        )
    pl.semaphore_wait(barrier, 4 + NF - 1)

    def weight_copy(half, k, source):
        return pltpu.make_async_remote_copy(
            src_ref=wb.at[source, :, pl.ds(half * 2 * width, 2 * width)],
            dst_ref=wb.at[source, :, pl.ds(half * 2 * width, 2 * width)],
            send_sem=w_send.at[half, k - 1],
            recv_sem=w_recv.at[half, k - 1],
            device_id={"feat": lax.rem(feat + k, NF), "rows": place},
            device_id_type=MESH,
        )

    def weights_start(half):
        for k in range(1, NF):
            weight_copy(half, k, feat).start()

    def weights_wait(half):
        for k in range(1, NF):
            weight_copy(half, k, lax.rem(feat - k + NF, NF)).wait_recv()

    half_pairs = features // 4
    plans = (tree(NX, NZ), tree(NZ, NX))
    sends = []

    def block(kind, i, j):
        dz, dx = (j, i) if kind == 0 else (i, j)
        return gat.at[pl.ds(kind * half_pairs, half_pairs), at(dz, dx)]

    def number(kind, i, j):
        dz, dx = (j, i) if kind == 0 else (i, j)
        return (dz % NZ) * NX + dx % NX

    def block_copy(kind, i, j, child):
        axis, step, ci, cj = child
        along_x = (axis == 0) == (kind == 0)
        n = number(kind, ci, cj)
        return pltpu.make_async_remote_copy(
            src_ref=block(kind, i, j),
            dst_ref=block(kind, i, j),
            send_sem=g_send.at[kind, n],
            recv_sem=g_recv.at[kind, n],
            device_id={"feat": feat, "rows": at(0, step) if along_x else at(step, 0)},
            device_id_type=MESH,
        )

    def gather_depth(depth):
        events = [[e for e in plan if e[0] == depth] for plan in plans]
        merged = []
        for n in range(max(len(e) for e in events)):
            for kind in (0, 1):
                if n < len(events[kind]):
                    merged.append((kind, events[kind][n]))
        for kind, (_, i, j, children) in merged:
            if depth > 0:
                n = number(kind, i, j)
                pltpu.make_async_remote_copy(
                    src_ref=block(kind, i, j),
                    dst_ref=block(kind, i, j),
                    send_sem=g_send.at[kind, n],
                    recv_sem=g_recv.at[kind, n],
                    device_id={"feat": feat, "rows": at(1, 0)},
                    device_id_type=MESH,
                ).wait_recv()
            for child in children:
                copy = block_copy(kind, i, j, child)
                copy.start()
                sends.append(copy)

    gather_depth(0)
    weights_start(0)
    weights_start(1)
    gather_depth(1)
    weights_wait(0)
    wt = wb[:, :, : 2 * width].reshape(width, 2 * width).T
    hi, lo = split(wt)
    wkv[...] = jnp.concatenate([hi, lo, hi, lo], axis=1)
    gather_depth(2)

    def keys_values(f, c):
        pltpu.make_async_copy(x_hbm.at[f], xb.at[f], x_sem.at[f]).wait()
        xh, xl_ = split(xb[f])
        kv = jnp.dot(
            wkv[...],
            jnp.concatenate([xh, xh, xl_, xl_], axis=0),
            preferred_element_type=F32,
        )
        kh, kl = split(kv[:width])
        vh, vl = split(kv[width:])
        for h in range(HEADS):
            s = slice(h * HEAD, (h + 1) * HEAD)
            kp[f, h] = jnp.concatenate([kh[s], kh[s], kl[s], kl[s]], axis=0).T
            vp[f, h] = jnp.concatenate([vh[s], vl[s], jnp.ones((16, rows), BF)], axis=0)
        return c

    quarter = features // 4
    for q in range(4):
        lax.fori_loop(q * quarter, (q + 1) * quarter, keys_values, 0)
        gather_depth(3 + q)

    weights_wait(1)
    wt = wb[:, :, 2 * width :].reshape(width, 2 * width)
    hi, lo = split(wt[:, :width].T)
    wqc[...] = jnp.concatenate([hi, lo, hi, lo], axis=1)
    hi, lo = split(wt[:, width:])
    woc[0] = hi
    woc[1] = lo

    def project_queries(p, c):
        both = gat[p].reshape(tests, 2 * width).T
        for u in range(2):
            th, tl = split(both[u * width : (u + 1) * width])
            q = jnp.dot(
                wqc[...], jnp.concatenate([th, th, tl, tl], axis=0), preferred_element_type=F32
            ) * (HEAD**-0.5 * LOG2E)
            qh, ql = split(q)
            for h in range(HEADS):
                s = slice(h * HEAD, (h + 1) * HEAD)
                qp[2 * p + u, h] = jnp.concatenate([qh[s], ql[s], qh[s], ql[s]], axis=0)
        return c

    lax.fori_loop(0, features // 2, project_queries, 0)

    def attend(f, c):
        u = lax.rem(f, GROUP)
        for h in range(HEADS):
            s = jnp.dot(kp[f, h], qp[f, h], preferred_element_type=F32)
            m = jnp.max(s, axis=0, keepdims=True)
            ph, pl_ = split(jnp.exp2(s - m))
            vv = vp[f, h]
            o = jnp.dot(vv, ph, preferred_element_type=F32) + jnp.dot(
                vv, pl_, preferred_element_type=F32
            )
            row = pl.multiple_of(u * width, 8) + h * HEAD
            ot[pl.ds(row, HEAD), :] = o[:HEAD] + o[HEAD : 2 * HEAD]
            ot[pl.ds(GROUP * width + u * HEADS + h, 1), :] = m
            ot[pl.ds(GROUP * width + (GROUP + u) * HEADS + h, 1), :] = o[2 * HEAD : 2 * HEAD + 1]
        return c

    stat0 = GROUP * width - (WIDE - 128)
    stats = GROUP * HEADS

    def spread_index(tile, n):
        lane = lax.broadcasted_iota(jnp.int32, (n, 128), 1)
        if tile < WIDE // 128 - 1:
            return stat0 + (lane + tile * 128) // HEAD
        low = stat0 + (lane + tile * 128) // HEAD
        high = stat0 + lane - (stat0 + stats)
        return jnp.where(lane < stat0, low, jnp.clip(high, 0, 127))

    def spread(factor, tile):
        idx = spread_index(tile, factor.shape[0])
        return jnp.take_along_axis(factor, idx, axis=1, mode="promise_in_bounds")

    def merge(dst, srcs, n):
        tail = pl.ds(WIDE - 128, 128)
        mine = dst[:, :, tail].reshape(n * 8, 128)
        theirs = [s[:, :, tail].reshape(n * 8, 128) for s in srcs]
        top = functools.reduce(jnp.maximum, theirs, mine)
        factors = [jnp.exp2(v - top) for v in (mine, *theirs)]
        lane = lax.broadcasted_iota(jnp.int32, (n * 8, 128), 1)
        is_max = (lane >= stat0) & (lane < stat0 + stats)
        for tile in range(WIDE // 128):
            at_ = pl.ds(tile * 128, 128)
            total = None
            for ref, factor in zip((dst, *srcs), factors):
                term = ref[:, :, at_].reshape(n * 8, 128) * spread(factor, tile)
                total = term if total is None else total + term
            if tile == WIDE // 128 - 1:
                total = jnp.where(is_max, top, total)
            dst[:, :, at_] = total.reshape(n, 8, 128)

    def column(g, dz):
        return own.at[g, pl.ds(lax.rem(z + dz + NZ, NZ) * NX, NX)]

    def cell(g, dx):
        return own.at[g, pl.ds(at(0, dx), 1)]

    def reduce_copy(g, n, src, dst, dz, dx):
        return pltpu.make_async_remote_copy(
            src_ref=src,
            dst_ref=dst,
            send_sem=r_send.at[g, n],
            recv_sem=r_recv.at[g, n],
            device_id={"feat": feat, "rows": at(dz, dx)},
            device_id_type=MESH,
        )

    def z_right(g, s):
        return reduce_copy(g, s, column(g, 4 - s), zr.at[g, s], 1, 0)

    def z_left(g, s):
        return reduce_copy(g, 4 + s, column(g, s - 3), zl.at[g, s], -1, 0)

    def x_right(g, s):
        return reduce_copy(g, 7 + s, cell(g, 2 - s), xr.at[g, s], 0, 1)

    def x_left(g):
        return reduce_copy(g, 9, cell(g, -1), xl.at[g], 0, -1)

    def start(copy):
        copy.start()
        sends.append(copy)

    def tick(g, s):
        if s == 0:
            own[g] = ot[...].T.reshape(own.shape[1:])
            start(z_right(g, 0))
            start(z_left(g, 0))
        elif s <= 3:
            z_right(g, s - 1).wait_recv()
            merge(column(g, 4 - s), [zr.at[g, s - 1]], NX)
            start(z_right(g, s))
            if s <= 2:
                z_left(g, s - 1).wait_recv()
                merge(column(g, s - 3), [zl.at[g, s - 1]], NX)
                start(z_left(g, s))
        elif s == 4:
            z_left(g, 2).wait_recv()
            z_right(g, 3).wait_recv()
            merge(column(g, 0), [zr.at[g, 3], zl.at[g, 2]], NX)
            start(x_right(g, 0))
            start(x_left(g))
        elif s == 5:
            x_right(g, 0).wait_recv()
            merge(cell(g, 1), [xr.at[g, 0]], 1)
            start(x_right(g, 1))
        elif s == 6:
            x_left(g).wait_recv()
            x_right(g, 1).wait_recv()
            merge(cell(g, 0), [xr.at[g, 1], xl.at[g]], 1)

    groups = features // GROUP
    progress = [0] * groups

    def tick_all(upto):
        for g in range(upto):
            if progress[g] <= 6:
                tick(g, progress[g])
                progress[g] += 1

    for g in range(groups):
        if g == 0:
            lax.fori_loop(0, GROUP, attend, 0)
        else:
            lax.fori_loop(g * GROUP, g * GROUP + 2, attend, 0)
            tick_all(g)
            lax.fori_loop(g * GROUP + 2, (g + 1) * GROUP, attend, 0)
        tick_all(g + 1)
    while min(progress) <= 6:
        tick_all(groups)

    wh, wl = woc[0], woc[1]
    for g in range(groups):
        mine = own.at[g, place]
        inverse = 1.0 / mine[:, WIDE - 128 :]
        parts = []
        for tile in range(WIDE // 128):
            index = spread_index(tile, 8) + stats
            if tile == WIDE // 128 - 1:
                index = jnp.clip(index, 0, 127)
            scale = jnp.take_along_axis(inverse, index, axis=1, mode="promise_in_bounds")
            parts.append(mine[:, tile * 128 : (tile + 1) * 128] * scale)
        mixed = jnp.concatenate(parts, axis=1)
        for u in range(GROUP):
            mh, ml = split(mixed[:, u * width : (u + 1) * width])
            out_ref[g * GROUP + u] = (
                jnp.dot(mh, wh, preferred_element_type=F32)
                + jnp.dot(mh, wl, preferred_element_type=F32)
                + jnp.dot(ml, wh, preferred_element_type=F32)
                + jnp.dot(ml, wl, preferred_element_type=F32)
            )
    for half in range(2):
        for k in range(1, NF):
            weight_copy(half, k, feat).wait_send()
    for copy in sends:
        copy.wait_send()


def per_device(test_cells, train_cells, w_query, w_key, w_value, w_out):
    cells = jnp.transpose(train_cells, (1, 2, 0))
    tests = jnp.transpose(test_cells, (1, 0, 2))
    features, width, rows = cells.shape
    mine = tests.shape[1]
    owners = NZ * NX
    all_tests = owners * mine
    groups = features // GROUP
    vmem = pl.BlockSpec(memory_space=pltpu.VMEM)
    dma = pltpu.SemaphoreType.DMA
    out = pl.pallas_call(
        kernel,
        out_shape=jax.ShapeDtypeStruct((features, mine, width), F32),
        in_specs=[pl.BlockSpec(memory_space=pl.ANY)] + [vmem] * 5,
        out_specs=vmem,
        scratch_shapes=[
            pltpu.VMEM((features, width, rows), F32),
            pltpu.VMEM((NF, width // NF, 4 * width), F32),
            pltpu.VMEM((features // 2, owners, mine, 2 * width), F32),
            pltpu.VMEM((features, HEADS, rows, 4 * HEAD), BF),
            pltpu.VMEM((features, HEADS, VROWS, rows), BF),
            pltpu.VMEM((features, HEADS, 4 * HEAD, all_tests), BF),
            pltpu.VMEM((2 * width, 4 * width), BF),
            pltpu.VMEM((width, 4 * width), BF),
            pltpu.VMEM((2, width, width), BF),
            pltpu.VMEM((WIDE, all_tests), F32),
            pltpu.VMEM((groups, owners, mine, WIDE), F32),
            pltpu.VMEM((groups, 4, NX, mine, WIDE), F32),
            pltpu.VMEM((groups, 3, NX, mine, WIDE), F32),
            pltpu.VMEM((groups, 2, 1, mine, WIDE), F32),
            pltpu.VMEM((groups, 1, mine, WIDE), F32),
            dma((features,)),
            dma((2, NF - 1)),
            dma((2, NF - 1)),
            dma((2, owners)),
            dma((2, owners)),
            dma((groups, 10)),
            dma((groups, 10)),
        ],
        compiler_params=pltpu.CompilerParams(
            collective_id=0, has_side_effects=True, vmem_limit_bytes=60 * 2**20
        ),
        name="attention",
    )(cells, tests, w_query, w_key, w_value, w_out)
    return jnp.transpose(out, (1, 0, 2))


def solution(mesh):
    rows = P("rows", "feat", None)
    weights = P("feat", None)
    return jax.shard_map(
        per_device,
        mesh=mesh,
        in_specs=(rows, rows, weights, weights, weights, weights),
        out_specs=rows,
        check_vma=False,
    )
```

time: 409 us -> 98.1 us (0.24)
  blocking collectives: 184 us -> 0 us
  Pallas kernels: 0 us -> 96.4 us
  matrix products: 87.3 us -> 0 us
  local copies, waits for them, and re-layouts: 49.2 us -> 1.54 us
  waiting for transfers between devices: 32.1 us -> 0 us
  loops' own time: 23.3 us -> 0 us
  other arithmetic: 17.8 us -> 0 us
  between operations: 13.6 us -> 0.01 us
    all_to_all x2 -> x0, blocking collectives: 157 us -> none  [the longest x1 80 us: sent_to_all(): return lax.all_to_all(copies, axis, split_axis=0, concat_axis=0, tiled=True)]
    pallas_call x0 -> x1, Pallas kernels: none -> 96.4 us  [per_device(): pl.pallas_call(kernel, out_shape=jax.ShapeDtypeStruct((features, mine, wi...]
    dot_general x28 -> x0, matrix products: 87.3 us -> none  [the longest x12 37.1 us: one_feature(): weighted = jnp.einsum('hqk,khe->qhe', probs, value_part, precision=highest)]
    dynamic_slice x48 -> x0, local copies, waits for them, and re-layouts: 32.7 us -> none  [the longest x12 12.3 us: one_feature(): lax.dynamic_index_in_dim(key_rows, feature, 1, keepdims=False)]
    all_gather x1 -> x0, waiting for transfers between devices: 32 us -> none  [whole_of(): out = lax.all_gather(out, axes[number], axis=dim, tiled=True)]
    all_gather x2 -> x0, blocking collectives: 27 us -> none  [the longest x1 13.7 us: in_one_piece(): out = lax.all_gather(both, axis, axis=dim, tiled=True)]
    another operation x1 -> x0, loops' own time: 23.3 us -> none  [per_device(): lax.map(one_feature, jnp.arange(features, dtype=jnp.int32))]
    reduce_sum x13 -> x0, other arithmetic: 11.3 us -> none  [the longest x12 11.1 us: one_feature(): totals = jnp.sum(probs, axis=-1)]
  transfers between devices with their start and end apart: 1 -> 0, of which waited for: 1 -> 0; matrix products, arithmetic and copies ran while one was open for 4% -> 0% of each run, Pallas kernels for 0% -> 0%
where the time goes in v1:
time: 98.1 us; the launch traced here: 98 us
  Pallas kernels  96.4 us (98%)
  local copies, waits for them, and re-layouts  1.54 us (2%)
    pallas_call x1, Pallas kernels, per_device(): pl.pallas_call(kernel, out_shape=jax.ShapeDtypeStruct((features, mine, wi...  96.4 us

profile of v1, /device:TPU:2, one launch (start us, length us, event | category | flops | bytes accessed | tf_op | source)
XLA Modules:
  0.0 98.0 jit_solution(13653457224006511878)
XLA Ops:
  0.0 96.4 %attention.1 = f32[12,8,192]{2,1,0:T(8,128)} custom-call(f32[12,192,512]{2,1,0:T(8,128)} %bitcast.3, f32[12,8,192]{2,1,0:T(8,128)} %bitcast.5, f32[24,192]{1,0:T(8,128)} %wq_ref.1, f32[24,192]{1,0:T(8,128)} %wk_ref.1, f32[24,192]{1,0:T(8,128)} %wv_ref.1, f32[24,192]{1,0:T(8,128)} %wo_ref.1), custom_call_target="tpu_custom_call" | custom-call | tf_op jit(solution)/shard_map/attention/pallas_call | solution.py:369
  96.4 1.5 %copy.8 = f32[8,12,192]{2,0,1:T(8,128)} copy(f32[8,12,192]{2,0,1:T(8,128)} %bitcast.4) | data formatting | bytes 147456

commit v2 on v0

v2 whole, which is shorter than its diff:
```python
import functools

import jax
import jax.numpy as jnp
from jax import lax
from jax.experimental import pallas as pl
from jax.experimental.pallas import tpu as pltpu
from jax.sharding import PartitionSpec as P

BF = jnp.bfloat16
F32 = jnp.float32
HEADS = 6
HEAD = 32
LOG2E = 1.4426950408889634
NZ, NX, NF = 8, 4, 8
VROWS = 2 * HEAD + 16
GROUPS = (3, 3, 2, 2, 1, 1)
Z_FIRST = 2
MESH = pl.DeviceIdType.MESH


def split(x):
    hi = x.astype(BF)
    return hi, (x - hi.astype(F32)).astype(BF)


def lanes(count):
    return -(-count * HEADS * (HEAD + 2) // 128) * 128


def kernel(
    x_hbm, t_ref, wq_ref, wk_ref, wv_ref, wo_ref, out_ref,
    xb, wb, gat, kp, vp, qp, wkv, wqc, woc, ot,
    x_sem, w_send, w_recv, g_send, g_recv, r_send, r_recv, own, inbox,
):
    width = HEADS * HEAD
    features = x_hbm.shape[0]
    rows = x_hbm.shape[2]
    tests = gat.shape[1] * gat.shape[2] * gat.shape[3]
    feat, place = lax.axis_index("feat"), lax.axis_index("rows")
    z, x = place // NX, place % NX
    nothing = place // (NZ * NX)

    def at(dz, dx):
        return lax.rem(z + dz + NZ, NZ) * NX + lax.rem(x + dx + NX, NX)

    for f in range(features):
        pltpu.make_async_copy(x_hbm.at[f], xb.at[f], x_sem.at[f]).start()

    wb[0, feat] = jnp.concatenate([wk_ref[...], wv_ref[...]], axis=1)
    wb[1, feat] = jnp.concatenate([wq_ref[...], wo_ref[...]], axis=1)
    pairs = features // 2
    for p in range(pairs):
        gat[p, z, x] = jnp.concatenate([t_ref[2 * p], t_ref[2 * p + 1]], axis=1)

    def there(dz, dx):
        return {"feat": feat, "rows": at(dz, dx)}

    def peer(k):
        return {"feat": lax.rem(feat + k, NF), "rows": place}

    with jax.named_scope("bar"):
        barrier = pltpu.get_barrier_semaphore()
        peers = [there(dz, 0) for dz in range(1, NZ)] + [there(0, 1), there(0, -1)]
        peers += [peer(k) for k in range(1, NF)]
        for other in peers:
            pl.semaphore_signal(barrier, inc=1, device_id=other, device_id_type=MESH)
        pl.semaphore_wait(barrier, len(peers))

    def remote(src, dst, send_sem, recv_sem, device):
        return pltpu.make_async_remote_copy(
            src_ref=src,
            dst_ref=dst,
            send_sem=send_sem,
            recv_sem=recv_sem,
            device_id=device,
            device_id_type=MESH,
        )

    def weights_start(half):
        for k in range(1, NF):
            mine = wb.at[half, feat]
            remote(mine, mine, w_send.at[half], w_recv.at[half], peer(k)).start()

    def weights_all(half):
        seven = wb.at[half, pl.ds(0, NF - 1)]
        return remote(seven, seven, w_send.at[half], w_recv.at[half], peer(1))

    def stage(p, n, ref, device):
        return remote(ref, ref, g_send.at[p, n], g_recv.at[p, n], device)

    def stage_all(p, n):
        ref = (gat.at[p, pl.ds(0, NZ - 1), 0], gat.at[p, pl.ds(0, 4)], gat.at[p, pl.ds(0, 2)])[n]
        return stage(p, n, ref, there(1, 0))

    def column_of(dx):
        return lax.rem(x + dx + NX, NX)

    def along_z(p):
        for dz in range(1, NZ):
            stage(p, 0, gat.at[p, z, x], there(dz, 0)).start()

    def along_x(p):
        with jax.named_scope("x1_%d" % p):
            stage_all(p, 0).wait_recv()
        for dx in (1, -1):
            stage(p, 1, gat.at[p, :, x], there(0, dx)).start()

    def further_x(p):
        with jax.named_scope("x2_%d" % p):
            stage_all(p, 1).wait_recv()
        half = NZ // 2
        stage(p, 2, gat.at[p, pl.ds(0, half), column_of(-1)], there(0, 1)).start()
        stage(p, 2, gat.at[p, pl.ds(half, half), column_of(1)], there(0, -1)).start()

    def arrived(p):
        with jax.named_scope("x3_%d" % p):
            stage_all(p, 2).wait_recv()

    weights_start(0)
    for p in range(pairs):
        along_z(p)
    along_x(0)
    with jax.named_scope("w0"):
        weights_all(0).wait_recv()
    weights_start(1)
    hi, lo = split(wb[0].reshape(width, 2 * width).T)
    wkv[...] = jnp.concatenate([hi, lo, hi, lo], axis=1)

    def keys_values(f, c):
        pltpu.make_async_copy(x_hbm.at[f], xb.at[f], x_sem.at[f]).wait()
        xh, xl_ = split(xb[f])
        kv = jnp.dot(
            wkv[...],
            jnp.concatenate([xh, xh, xl_, xl_], axis=0),
            preferred_element_type=F32,
        )
        kh, kl = split(kv[:width])
        vh, vl = split(kv[width:])
        for h in range(HEADS):
            s = slice(h * HEAD, (h + 1) * HEAD)
            kp[f, h] = jnp.concatenate([kh[s], kh[s], kl[s], kl[s]], axis=0).T
            vp[f, h] = jnp.concatenate([vh[s], vl[s], jnp.ones((16, rows), BF)], axis=0)
        return c

    moves = [
        [(along_x, 1)],
        [(further_x, 0), (along_x, 2)],
        [(along_x, 3)],
        [(further_x, 1)],
        [(along_x, 4)],
        [(further_x, 2), (along_x, 5)],
    ]
    for p in range(pairs):
        with jax.named_scope("kv"):
            lax.fori_loop(2 * p, 2 * p + 2, keys_values, 0)
        for move, n in moves[p]:
            move(n)

    with jax.named_scope("w1"):
        weights_all(1).wait_recv()
    wt = wb[1].reshape(width, 2 * width)
    hi, lo = split(wt[:, :width].T)
    wqc[...] = jnp.concatenate([hi, lo, hi, lo], axis=1)
    hi, lo = split(wt[:, width:])
    woc[0] = hi
    woc[1] = lo

    def project_queries(p):
        arrived(p)
        both = gat[p].reshape(tests, 2 * width).T
        for u in range(2):
            th, tl = split(both[u * width : (u + 1) * width])
            q = jnp.dot(
                wqc[...], jnp.concatenate([th, th, tl, tl], axis=0), preferred_element_type=F32
            ) * (HEAD**-0.5 * LOG2E)
            qh, ql = split(q)
            for h in range(HEADS):
                s = slice(h * HEAD, (h + 1) * HEAD)
                qp[2 * p + u, h] = jnp.concatenate([qh[s], ql[s], qh[s], ql[s]], axis=0)

    def attend(first, count, f):
        u = f - first
        for h in range(HEADS):
            s = jnp.dot(kp[f, h], qp[f, h], preferred_element_type=F32)
            m = jnp.max(s, axis=0, keepdims=True)
            ph, pl_ = split(jnp.exp2(s - m))
            vv = vp[f, h]
            o = jnp.dot(vv, ph, preferred_element_type=F32) + jnp.dot(
                vv, pl_, preferred_element_type=F32
            )
            row = pl.multiple_of(u * width, 8) + h * HEAD
            ot[pl.ds(row, HEAD), :] = o[:HEAD] + o[HEAD : 2 * HEAD]
            ot[pl.ds(count * width + u * HEADS + h, 1), :] = m
            ot[pl.ds(count * width + (count + u) * HEADS + h, 1), :] = o[2 * HEAD : 2 * HEAD + 1]

    def spread_index(count, tile, n):
        lane = lax.broadcasted_iota(jnp.int32, (n, 128), 1)
        wide = lanes(count)
        first = count * width - (wide - 128)
        low = first + (lane + tile * 128) // HEAD
        if tile < wide // 128 - 1:
            return low
        high = lane - count * HEADS
        return jnp.clip(jnp.where(lane < first, low, high), 0, 127)

    def merge(count, dst, srcs):
        wide = lanes(count)
        first = count * width - (wide - 128)
        shape = dst.shape[:-1]
        n = dst.size // wide
        tail = pl.ds(wide - 128, 128)

        def load(ref, part):
            return ref[..., part].reshape(n, 128)

        refs = (dst, *srcs)
        stats = [load(r, tail) for r in refs]
        top = functools.reduce(jnp.maximum, stats)
        factors = [jnp.exp2(v - top) for v in stats]
        lane = lax.broadcasted_iota(jnp.int32, (n, 128), 1)
        is_max = (lane >= first) & (lane < first + count * HEADS)
        for tile in range(wide // 128):
            part = pl.ds(tile * 128, 128)
            index = spread_index(count, tile, n)
            total = None
            for ref, factor in zip(refs, factors):
                scale = jnp.take_along_axis(factor, index, axis=1, mode="promise_in_bounds")
                term = load(ref, part) * scale
                total = term if total is None else total + term
            if tile == wide // 128 - 1:
                total = jnp.where(is_max, top, total)
            dst[..., part] = total.reshape(*shape, 128)

    def z_of(dz):
        return lax.rem(z + dz + NZ, NZ)

    def x_of(dx):
        return lax.rem(x + dx + NX, NX)

    def send(g, n, src, dst, dz, dx):
        remote(src, dst, r_send.at[g], r_recv.at[g, n], there(dz, dx)).start()

    def receive(g, n, dst):
        remote(dst, dst, r_send.at[g], r_recv.at[g, n], there(1, 0)).wait_recv()

    def z_first(g, s):
        count, mine = GROUPS[g], own[g]
        zr, zl, xr, xl = inbox[g]
        if s <= 3:
            if s > 0:
                receive(g, s - 1, zr.at[s - 1])
                merge(count, mine.at[z_of(4 - s)], [zr.at[s - 1]])
            send(g, s, mine.at[z_of(4 - s)], zr.at[s], 1, 0)
            if s < 3:
                if s > 0:
                    receive(g, 3 + s, zl.at[s - 1])
                    merge(count, mine.at[z_of(s - 3)], [zl.at[s - 1]])
                send(g, 4 + s, mine.at[z_of(s - 3)], zl.at[s], -1, 0)
        elif s == 4:
            receive(g, 6, zl.at[2])
            receive(g, 3, zr.at[3])
            merge(count, mine.at[z], [zr.at[3], zl.at[2]])
            send(g, 7, mine.at[z, x_of(2)], xr.at[0], 0, 1)
            send(g, 9, mine.at[z, x_of(-1)], xl, 0, -1)
        elif s == 5:
            receive(g, 7, xr.at[0])
            merge(count, mine.at[z, x_of(1)], [xr.at[0]])
            send(g, 8, mine.at[z, x_of(1)], xr.at[1], 0, 1)
        else:
            receive(g, 9, xl)
            receive(g, 8, xr.at[1])
            merge(count, mine.at[z, x], [xr.at[1], xl])

    def x_first(g, s):
        count, mine = GROUPS[g], own[g]
        half, right, left, rest = inbox[g]
        low, high = pl.ds(0, NZ // 2), pl.ds(NZ // 2, NZ // 2)
        if s == 0:
            send(g, 0, mine.at[low, x_of(2)], half.at[0], 0, 1)
            send(g, 1, mine.at[high, x_of(2)], half.at[1], 0, -1)
        elif s == 1:
            receive(g, 0, half.at[0])
            merge(count, mine.at[low, x_of(1)], [half.at[0]])
            send(g, 2, mine.at[:, x_of(1)], right, 0, 1)
            receive(g, 1, half.at[1])
            merge(count, mine.at[high, x_of(-1)], [half.at[1]])
            send(g, 3, mine.at[:, x_of(-1)], left, 0, -1)
        elif s == 2:
            receive(g, 2, right)
            receive(g, 3, left)
            merge(count, mine.at[:, x], [right, left])
            for dz in (4, 3, 5, 2, 6, 1, 7):
                send(g, 4, mine.at[z_of(dz), x], rest.at[dz - 1], dz, 0)
        else:
            receive(g, 4, rest)
            merge(count, mine.at[z, x], [rest.at[k] for k in range(NZ - 1)])

    starts = [sum(GROUPS[:g]) for g in range(len(GROUPS))]

    def finish(g):
        count = GROUPS[g]
        wide = lanes(count)
        mine = own[g].at[z, x]
        inverse = 1.0 / mine[:, wide - 128 :]
        parts = []
        for tile in range(wide // 128):
            index = jnp.clip(spread_index(count, tile, 8) + count * HEADS, 0, 127)
            scale = jnp.take_along_axis(inverse, index, axis=1, mode="promise_in_bounds")
            parts.append(mine[:, tile * 128 : (tile + 1) * 128] * scale)
        mixed = jnp.concatenate(parts, axis=1)
        for u in range(count):
            mh, ml = split(mixed[:, u * width : (u + 1) * width])
            out_ref[starts[g] + u] = (
                jnp.dot(mh, woc[0], preferred_element_type=F32)
                + jnp.dot(mh, woc[1], preferred_element_type=F32)
                + jnp.dot(ml, woc[0], preferred_element_type=F32)
                + jnp.dot(ml, woc[1], preferred_element_type=F32)
            )

    def tick(g, s):
        with jax.named_scope("t%d_%d" % (g, s)):
            if s == 0:
                own[g][...] = ot[: lanes(GROUPS[g]), :].T.reshape(own[g].shape)
            (z_first if g < Z_FIRST else x_first)(g, s)
            if s == (6 if g < Z_FIRST else 3):
                finish(g)

    def att(first, last):
        group = max(g for g in range(len(GROUPS)) if starts[g] <= first)

        def body(f, c):
            attend(starts[group], GROUPS[group], f)
            return c

        with jax.named_scope("att"):
            lax.fori_loop(first, last + nothing, body, 0)

    schedule = [
        (0, 2, []),
        (2, 3, [(0, 0)]),
        (3, 4, []),
        (4, 6, [(1, 0), (0, 1)]),
        (6, 8, [(2, 0), (0, 2), (1, 1)]),
        (8, 10, [(3, 0), (0, 3), (1, 2), (2, 1)]),
        (10, 11, [(4, 0), (0, 4), (3, 1)]),
        (11, 12, [(5, 0), (2, 2), (1, 3), (0, 5), (4, 1), (3, 2), (5, 1), (1, 4), (0, 6), (2, 3)]
         + [(4, 2), (5, 2), (1, 5), (3, 3), (4, 3), (1, 6), (5, 3)]),
    ]
    for first, last, ticks in schedule:
        if first % 2 == 0:
            p = first // 2
            if 0 < p < 4:
                further_x(p + 2)
            with jax.named_scope("pq"):
                project_queries(p)
        att(first, last)
        for g, s in ticks:
            tick(g, s)

    for half in range(2):
        weights_all(half).wait_send()
    for p in range(pairs):
        for n in range(3):
            stage_all(p, n).wait_send()
    for g in range(len(GROUPS)):
        sent = [own[g].at[pl.ds(0, 7)], own[g].at[0, pl.ds(0, 3)]]
        if g >= Z_FIRST:
            sent = [own[g].at[pl.ds(0, 6)], own[g].at[pl.ds(0, 7), 0]]
        for ref in sent:
            remote(ref, ref, r_send.at[g], r_recv.at[g, 0], there(1, 0)).wait_send()


def per_device(test_cells, train_cells, w_query, w_key, w_value, w_out):
    cells = jnp.transpose(train_cells, (1, 2, 0))
    tests = jnp.transpose(test_cells, (1, 0, 2))
    features, width, rows = cells.shape
    mine = tests.shape[1]
    owners = NZ * NX
    all_tests = owners * mine
    inboxes = []
    for g, count in enumerate(GROUPS):
        outer = [(4, NX), (3, NX), (2,), ()] if g < Z_FIRST else [(2, 4), (NZ,), (NZ,), (NZ - 1,)]
        inboxes.append([pltpu.VMEM((*o, mine, lanes(count)), F32) for o in outer])
    vmem = pl.BlockSpec(memory_space=pltpu.VMEM)
    dma = pltpu.SemaphoreType.DMA
    out = pl.pallas_call(
        kernel,
        out_shape=jax.ShapeDtypeStruct((features, mine, width), F32),
        in_specs=[pl.BlockSpec(memory_space=pl.ANY)] + [vmem] * 5,
        out_specs=vmem,
        scratch_shapes=[
            pltpu.VMEM((features, width, rows), F32),
            pltpu.VMEM((2, NF, width // NF, 2 * width), F32),
            pltpu.VMEM((features // 2, NZ, NX, mine, 2 * width), F32),
            pltpu.VMEM((features, HEADS, rows, 4 * HEAD), BF),
            pltpu.VMEM((features, HEADS, VROWS, rows), BF),
            pltpu.VMEM((features, HEADS, 4 * HEAD, all_tests), BF),
            pltpu.VMEM((2 * width, 4 * width), BF),
            pltpu.VMEM((width, 4 * width), BF),
            pltpu.VMEM((2, width, width), BF),
            pltpu.VMEM((lanes(max(GROUPS)), all_tests), F32),
            dma((features,)),
            dma((2,)),
            dma((2,)),
            dma((features // 2, 3)),
            dma((features // 2, 3)),
            dma((len(GROUPS),)),
            dma((len(GROUPS), 10)),
            [pltpu.VMEM((NZ, NX, mine, lanes(n)), F32) for n in GROUPS],
            inboxes,
        ],
        compiler_params=pltpu.CompilerParams(
            collective_id=0, has_side_effects=True, vmem_limit_bytes=60 * 2**20
        ),
        name="attention",
    )(cells, tests, w_query, w_key, w_value, w_out)
    return jnp.transpose(out, (1, 0, 2))


def solution(mesh):
    rows = P("rows", "feat", None)
    weights = P("feat", None)
    return jax.shard_map(
        per_device,
        mesh=mesh,
        in_specs=(rows, rows, weights, weights, weights, weights),
        out_specs=rows,
        check_vma=False,
    )
```

time: 409 us -> 73.3 us (0.18)
  blocking collectives: 184 us -> 0 us
  matrix products: 87.3 us -> 0 us
  Pallas kernels: 0 us -> 70.3 us
  local copies, waits for them, and re-layouts: 49.2 us -> 1.54 us
  waiting for transfers between devices: 32.1 us -> 0 us
  loops' own time: 23.3 us -> 0 us
  other arithmetic: 17.8 us -> 0 us
  between operations: 13.6 us -> 0.01 us
    all_to_all x2 -> x0, blocking collectives: 157 us -> none  [the longest x1 80 us: sent_to_all(): return lax.all_to_all(copies, axis, split_axis=0, concat_axis=0, tiled=True)]
    dot_general x28 -> x0, matrix products: 87.3 us -> none  [the longest x12 37.1 us: one_feature(): weighted = jnp.einsum('hqk,khe->qhe', probs, value_part, precision=highest)]
    pallas_call x0 -> x1, Pallas kernels: none -> 70.3 us  [per_device(): pl.pallas_call(kernel, out_shape=jax.ShapeDtypeStruct((features, mine, wi...]
    dynamic_slice x48 -> x0, local copies, waits for them, and re-layouts: 32.7 us -> none  [the longest x12 12.3 us: one_feature(): lax.dynamic_index_in_dim(key_rows, feature, 1, keepdims=False)]
    all_gather x1 -> x0, waiting for transfers between devices: 32 us -> none  [whole_of(): out = lax.all_gather(out, axes[number], axis=dim, tiled=True)]
    all_gather x2 -> x0, blocking collectives: 27 us -> none  [the longest x1 13.7 us: in_one_piece(): out = lax.all_gather(both, axis, axis=dim, tiled=True)]
    another operation x1 -> x0, loops' own time: 23.3 us -> none  [per_device(): lax.map(one_feature, jnp.arange(features, dtype=jnp.int32))]
    reduce_sum x13 -> x0, other arithmetic: 11.3 us -> none  [the longest x12 11.1 us: one_feature(): totals = jnp.sum(probs, axis=-1)]
  transfers between devices with their start and end apart: 1 -> 0, of which waited for: 1 -> 0; matrix products, arithmetic and copies ran while one was open for 4% -> 0% of each run, Pallas kernels for 0% -> 0%
where the time goes in v2:
time: 73.3 us; the launch traced here: 71.8 us
  Pallas kernels  70.3 us (96%)
  local copies, waits for them, and re-layouts  1.54 us (2%)
    pallas_call x1, Pallas kernels, per_device(): pl.pallas_call(kernel, out_shape=jax.ShapeDtypeStruct((features, mine, wi...  70.3 us
    unnamed x1, local copies, waits for them, and re-layouts  1.54 us

profile of v2, /device:TPU:2, one launch (start us, length us, event | category | flops | bytes accessed | tf_op | source)
XLA Modules:
  0.0 71.8 jit_solution(4849930020087630557)
XLA Ops:
  0.0 70.3 %attention.1 = f32[12,8,192]{2,1,0:T(8,128)} custom-call(f32[12,192,512]{2,1,0:T(8,128)} %bitcast.3, f32[12,8,192]{2,1,0:T(8,128)} %bitcast.5, f32[24,192]{1,0:T(8,128)} %wq_ref.1, f32[24,192]{1,0:T(8,128)} %wk_ref.1, f32[24,192]{1,0:T(8,128)} %wv_ref.1, f32[24,192]{1,0:T(8,128)} %wo_ref.1), custom_call_target="tpu_custom_call" | custom-call | tf_op jit(solution)/shard_map/attention/pallas_call | solution.py:387
  70.3 1.5 %copy.8 = f32[8,12,192]{2,0,1:T(8,128)} copy(f32[8,12,192]{2,0,1:T(8,128)} %bitcast.4) | data formatting | bytes 147456

commit v3 on v2

--- a/solution.py
+++ b/solution.py
@@ -13,9 +13,9 @@
 HEAD = 32
 LOG2E = 1.4426950408889634
 NZ, NX, NF = 8, 4, 8
-VROWS = 2 * HEAD + 16
+VROWS = 4 * HEAD + 16
 GROUPS = (3, 3, 2, 2, 1, 1)
-Z_FIRST = 2
+Z_FIRST = (0, 2)
 MESH = pl.DeviceIdType.MESH
 
 
@@ -30,7 +30,7 @@
 
 def kernel(
     x_hbm, t_ref, wq_ref, wk_ref, wv_ref, wo_ref, out_ref,
-    xb, wb, gat, kp, vp, qp, wkv, wqc, woc, ot,
+    xb, wb, gat, kp, vp, qp, wkv, wqc, woc, ot, kv, sc,
     x_sem, w_send, w_recv, g_send, g_recv, r_send, r_recv, own, inbox,
 ):
     width = HEADS * HEAD
@@ -127,33 +127,47 @@
     hi, lo = split(wb[0].reshape(width, 2 * width).T)
     wkv[...] = jnp.concatenate([hi, lo, hi, lo], axis=1)
 
-    def keys_values(f, c):
-        pltpu.make_async_copy(x_hbm.at[f], xb.at[f], x_sem.at[f]).wait()
+    def project(f, slot):
         xh, xl_ = split(xb[f])
-        kv = jnp.dot(
+        kv[slot] = jnp.dot(
             wkv[...],
             jnp.concatenate([xh, xh, xl_, xl_], axis=0),
             preferred_element_type=F32,
         )
-        kh, kl = split(kv[:width])
-        vh, vl = split(kv[width:])
+
+    def pack(f, slot):
+        kh, kl = split(kv[slot, :width])
+        vh, vl = split(kv[slot, width:])
         for h in range(HEADS):
             s = slice(h * HEAD, (h + 1) * HEAD)
             kp[f, h] = jnp.concatenate([kh[s], kh[s], kl[s], kl[s]], axis=0).T
-            vp[f, h] = jnp.concatenate([vh[s], vl[s], jnp.ones((16, rows), BF)], axis=0)
+        for g in range(HEADS // 2):
+            a = slice(2 * g * HEAD, (2 * g + 1) * HEAD)
+            b = slice((2 * g + 1) * HEAD, (2 * g + 2) * HEAD)
+            vp[f, g] = jnp.concatenate([vh[a], vl[a], vh[b], vl[b], jnp.ones((16, rows), BF)], axis=0)
+
+    def keys_values(p, c):
+        f = 2 * p
+        project(f + 1, 1)
+        pack(f, 0)
+        project(jnp.minimum(f + 2, features - 1), 0)
+        pack(f + 1, 1)
         return c
 
+    for f in range(features):
+        pltpu.make_async_copy(x_hbm.at[f], xb.at[f], x_sem.at[f]).wait()
+    project(0, 0)
     moves = [
         [(along_x, 1)],
+        [],
         [(further_x, 0), (along_x, 2)],
-        [(along_x, 3)],
-        [(further_x, 1)],
-        [(along_x, 4)],
-        [(further_x, 2), (along_x, 5)],
+        [],
+        [],
+        [(further_x, 1), (along_x, 3)],
     ]
     for p in range(pairs):
         with jax.named_scope("kv"):
-            lax.fori_loop(2 * p, 2 * p + 2, keys_values, 0)
+            lax.fori_loop(p, p + 1 + nothing, keys_values, 0)
         for move, n in moves[p]:
             move(n)
 
@@ -179,20 +193,38 @@
                 s = slice(h * HEAD, (h + 1) * HEAD)
                 qp[2 * p + u, h] = jnp.concatenate([qh[s], ql[s], qh[s], ql[s]], axis=0)
 
+    def scores(f, g):
+        for u in range(2):
+            h = 2 * g + u
+            sc[g, u] = jnp.dot(kp[f, h], qp[f, h], preferred_element_type=F32)
+
     def attend(first, count, f):
-        u = f - first
-        for h in range(HEADS):
-            s = jnp.dot(kp[f, h], qp[f, h], preferred_element_type=F32)
-            m = jnp.max(s, axis=0, keepdims=True)
-            ph, pl_ = split(jnp.exp2(s - m))
-            vv = vp[f, h]
-            o = jnp.dot(vv, ph, preferred_element_type=F32) + jnp.dot(
-                vv, pl_, preferred_element_type=F32
+        place_of = pl.multiple_of((f - first) * width, 8)
+        stat = count * width + (f - first) * HEADS
+        following = jnp.minimum(f + 1, features - 1)
+        pairs_of_heads = HEADS // 2
+        for g in range(pairs_of_heads):
+            if g + 1 < pairs_of_heads:
+                scores(f, g + 1)
+            else:
+                scores(following, 0)
+            tops = [jnp.max(sc[g, u], axis=0, keepdims=True) for u in range(2)]
+            probs = [split(jnp.exp2(sc[g, u] - tops[u])) for u in range(2)]
+            both = [jnp.concatenate([p[part] for p in probs], axis=1) for part in range(2)]
+            vv = vp[f, g]
+            o = jnp.dot(
+                jnp.concatenate([vv, vv], axis=1),
+                jnp.concatenate(both, axis=0),
+                preferred_element_type=F32,
             )
-            row = pl.multiple_of(u * width, 8) + h * HEAD
-            ot[pl.ds(row, HEAD), :] = o[:HEAD] + o[HEAD : 2 * HEAD]
-            ot[pl.ds(count * width + u * HEADS + h, 1), :] = m
-            ot[pl.ds(count * width + (count + u) * HEADS + h, 1), :] = o[2 * HEAD : 2 * HEAD + 1]
+            for u in range(2):
+                part = o[2 * u * HEAD : (2 * u + 2) * HEAD, u * tests : (u + 1) * tests]
+                h = 2 * g + u
+                ot[pl.ds(place_of + h * HEAD, HEAD), :] = part[:HEAD] + part[HEAD:]
+                ot[pl.ds(stat + h, 1), :] = tops[u]
+                ot[pl.ds(stat + count * HEADS + h, 1), :] = o[
+                    4 * HEAD : 4 * HEAD + 1, u * tests : (u + 1) * tests
+                ]
 
     def spread_index(count, tile, n):
         lane = lax.broadcasted_iota(jnp.int32, (n, 128), 1)
@@ -322,8 +354,8 @@
         with jax.named_scope("t%d_%d" % (g, s)):
             if s == 0:
                 own[g][...] = ot[: lanes(GROUPS[g]), :].T.reshape(own[g].shape)
-            (z_first if g < Z_FIRST else x_first)(g, s)
-            if s == (6 if g < Z_FIRST else 3):
+            (z_first if g in Z_FIRST else x_first)(g, s)
+            if s == (6 if g in Z_FIRST else 3):
                 finish(g)
 
     def att(first, last):
@@ -337,23 +369,24 @@
             lax.fori_loop(first, last + nothing, body, 0)
 
     schedule = [
-        (0, 2, []),
-        (2, 3, [(0, 0)]),
-        (3, 4, []),
-        (4, 6, [(1, 0), (0, 1)]),
-        (6, 8, [(2, 0), (0, 2), (1, 1)]),
-        (8, 10, [(3, 0), (0, 3), (1, 2), (2, 1)]),
-        (10, 11, [(4, 0), (0, 4), (3, 1)]),
-        (11, 12, [(5, 0), (2, 2), (1, 3), (0, 5), (4, 1), (3, 2), (5, 1), (1, 4), (0, 6), (2, 3)]
-         + [(4, 2), (5, 2), (1, 5), (3, 3), (4, 3), (1, 6), (5, 3)]),
+        (0, 1, [(project_queries, 0)], []),
+        (1, 3, [(further_x, 2), (along_x, 4), (project_queries, 1)], [(0, 0)]),
+        (3, 5, [(further_x, 3), (along_x, 5), (project_queries, 2)], [(0, 1)]),
+        (5, 6, [(further_x, 4), (project_queries, 3)], [(1, 0)]),
+        (6, 7, [(further_x, 5)], [(0, 2)]),
+        (7, 8, [(project_queries, 4)], [(2, 0), (1, 1)]),
+        (8, 9, [], [(0, 3)]),
+        (9, 10, [(project_queries, 5)], [(3, 0), (2, 1)]),
+        (10, 11, [], [(4, 0), (1, 2), (0, 4)]),
+        (11, 12, [],
+         [(5, 0), (2, 2), (3, 1), (0, 5), (4, 1), (5, 1), (2, 3), (0, 6), (3, 2), (4, 2), (1, 3)]
+         + [(2, 4), (5, 2), (2, 5), (3, 3), (4, 3), (2, 6), (5, 3)]),
     ]
-    for first, last, ticks in schedule:
-        if first % 2 == 0:
-            p = first // 2
-            if 0 < p < 4:
-                further_x(p + 2)
-            with jax.named_scope("pq"):
-                project_queries(p)
+    for first, last, before, ticks in schedule:
+        for act, n in before:
+            act(n)
+        if first == 0:
+            scores(0, 0)
         att(first, last)
         for g, s in ticks:
             tick(g, s)
@@ -365,7 +398,7 @@
             stage_all(p, n).wait_send()
     for g in range(len(GROUPS)):
         sent = [own[g].at[pl.ds(0, 7)], own[g].at[0, pl.ds(0, 3)]]
-        if g >= Z_FIRST:
+        if g not in Z_FIRST:
             sent = [own[g].at[pl.ds(0, 6)], own[g].at[pl.ds(0, 7), 0]]
         for ref in sent:
             remote(ref, ref, r_send.at[g], r_recv.at[g, 0], there(1, 0)).wait_send()
@@ -380,7 +413,7 @@
     all_tests = owners * mine
     inboxes = []
     for g, count in enumerate(GROUPS):
-        outer = [(4, NX), (3, NX), (2,), ()] if g < Z_FIRST else [(2, 4), (NZ,), (NZ,), (NZ - 1,)]
+        outer = [(4, NX), (3, NX), (2,), ()] if g in Z_FIRST else [(2, 4), (NZ,), (NZ,), (NZ - 1,)]
         inboxes.append([pltpu.VMEM((*o, mine, lanes(count)), F32) for o in outer])
     vmem = pl.BlockSpec(memory_space=pltpu.VMEM)
     dma = pltpu.SemaphoreType.DMA
@@ -394,12 +427,14 @@
             pltpu.VMEM((2, NF, width // NF, 2 * width), F32),
             pltpu.VMEM((features // 2, NZ, NX, mine, 2 * width), F32),
             pltpu.VMEM((features, HEADS, rows, 4 * HEAD), BF),
-            pltpu.VMEM((features, HEADS, VROWS, rows), BF),
+            pltpu.VMEM((features, HEADS // 2, VROWS, rows), BF),
             pltpu.VMEM((features, HEADS, 4 * HEAD, all_tests), BF),
             pltpu.VMEM((2 * width, 4 * width), BF),
             pltpu.VMEM((width, 4 * width), BF),
             pltpu.VMEM((2, width, width), BF),
             pltpu.VMEM((lanes(max(GROUPS)), all_tests), F32),
+            pltpu.VMEM((2, 2 * width, rows), F32),
+            pltpu.VMEM((HEADS // 2, 2, rows, all_tests), F32),
             dma((features,)),
             dma((2,)),
             dma((2,)),

time: 73.3 us -> 69.7 us (0.951); the launches traced: 71.8 us -> 69.1 us
  Pallas kernels: 70.3 us -> 67.5 us
    pallas_call x1, Pallas kernels: 70.3 us -> 67.5 us  [per_device(): pl.pallas_call(kernel, out_shape=jax.ShapeDtypeStruct((features, mine, wi...]
where the time goes in v3:
time: 69.7 us; the launch traced here: 69.1 us
  Pallas kernels  67.5 us (97%)
  local copies, waits for them, and re-layouts  1.54 us (2%)
    pallas_call x1, Pallas kernels, per_device(): pl.pallas_call(kernel, out_shape=jax.ShapeDtypeStruct((features, mine, wi...  67.5 us
    unnamed x1, local copies, waits for them, and re-layouts  1.54 us

profile of v3, /device:TPU:2, one launch (start us, length us, event | category | flops | bytes accessed | tf_op | source)
XLA Modules:
  0.0 69.1 jit_solution(11952154597635822955)
XLA Ops:
  0.0 67.5 %attention.1 = f32[12,8,192]{2,1,0:T(8,128)} custom-call(f32[12,192,512]{2,1,0:T(8,128)} %bitcast.3, f32[12,8,192]{2,1,0:T(8,128)} %bitcast.5, f32[24,192]{1,0:T(8,128)} %wq_ref.1, f32[24,192]{1,0:T(8,128)} %wk_ref.1, f32[24,192]{1,0:T(8,128)} %wv_ref.1, f32[24,192]{1,0:T(8,128)} %wo_ref.1), custom_call_target="tpu_custom_call" | custom-call | tf_op jit(solution)/shard_map/attention/pallas_call | solution.py:420
  67.5 1.5 %copy.8 = f32[8,12,192]{2,0,1:T(8,128)} copy(f32[8,12,192]{2,0,1:T(8,128)} %bitcast.4) | data formatting | bytes 147456

commit v4 on v3

--- a/solution.py
+++ b/solution.py
@@ -14,8 +14,9 @@
 LOG2E = 1.4426950408889634
 NZ, NX, NF = 8, 4, 8
 VROWS = 4 * HEAD + 16
+ROW_FIRST = (4, 5)
 GROUPS = (3, 3, 2, 2, 1, 1)
-Z_FIRST = (0, 2)
+Z_FIRST = (0,)
 MESH = pl.DeviceIdType.MESH
 
 
@@ -29,9 +30,9 @@
 
 
 def kernel(
-    x_hbm, t_ref, wq_ref, wk_ref, wv_ref, wo_ref, out_ref,
+    x_hbm, t_hbm, wq_hbm, wk_hbm, wv_hbm, wo_hbm, out_ref,
     xb, wb, gat, kp, vp, qp, wkv, wqc, woc, ot, kv, sc,
-    x_sem, w_send, w_recv, g_send, g_recv, r_send, r_recv, own, inbox,
+    x_sem, w_send, w_recv, g_send, g_recv, r_send, r_recv, own, inbox, t_ref, w_ref, in_sem,
 ):
     width = HEADS * HEAD
     features = x_hbm.shape[0]
@@ -44,27 +45,33 @@
     def at(dz, dx):
         return lax.rem(z + dz + NZ, NZ) * NX + lax.rem(x + dx + NX, NX)
 
+    def there(dz, dx):
+        return {"feat": feat, "rows": at(dz, dx)}
+
+    def peer(k):
+        return {"feat": lax.rem(feat + k, NF), "rows": place}
+
+    barrier = pltpu.get_barrier_semaphore()
+    peers = [there(dz, 0) for dz in range(1, NZ)] + [there(0, 1), there(0, -1)]
+    peers += [peer(k) for k in range(1, NF)]
+    for other in peers:
+        pl.semaphore_signal(barrier, inc=1, device_id=other, device_id_type=MESH)
+
+    small = [pltpu.make_async_copy(t_hbm, t_ref, in_sem.at[0])]
+    for n, w_hbm in enumerate((wk_hbm, wv_hbm, wq_hbm, wo_hbm)):
+        small.append(pltpu.make_async_copy(w_hbm, w_ref.at[n], in_sem.at[n + 1]))
+    for copy in small:
+        copy.start()
     for f in range(features):
         pltpu.make_async_copy(x_hbm.at[f], xb.at[f], x_sem.at[f]).start()
-
-    wb[0, feat] = jnp.concatenate([wk_ref[...], wv_ref[...]], axis=1)
-    wb[1, feat] = jnp.concatenate([wq_ref[...], wo_ref[...]], axis=1)
+    for copy in small:
+        copy.wait()
+    for half in range(2):
+        wb[half, feat] = jnp.concatenate([w_ref[2 * half], w_ref[2 * half + 1]], axis=1)
     pairs = features // 2
     for p in range(pairs):
         gat[p, z, x] = jnp.concatenate([t_ref[2 * p], t_ref[2 * p + 1]], axis=1)
-
-    def there(dz, dx):
-        return {"feat": feat, "rows": at(dz, dx)}
-
-    def peer(k):
-        return {"feat": lax.rem(feat + k, NF), "rows": place}
-
     with jax.named_scope("bar"):
-        barrier = pltpu.get_barrier_semaphore()
-        peers = [there(dz, 0) for dz in range(1, NZ)] + [there(0, 1), there(0, -1)]
-        peers += [peer(k) for k in range(1, NF)]
-        for other in peers:
-            pl.semaphore_signal(barrier, inc=1, device_id=other, device_id_type=MESH)
         pl.semaphore_wait(barrier, len(peers))
 
     def remote(src, dst, send_sem, recv_sem, device):
@@ -90,14 +97,43 @@
         return remote(ref, ref, g_send.at[p, n], g_recv.at[p, n], device)
 
     def stage_all(p, n):
-        ref = (gat.at[p, pl.ds(0, NZ - 1), 0], gat.at[p, pl.ds(0, 4)], gat.at[p, pl.ds(0, 2)])[n]
+        if p in ROW_FIRST:
+            ref = (
+                gat.at[p, 0, pl.ds(0, 2)],
+                gat.at[p, 0, pl.ds(0, 1)],
+                gat.at[p, pl.ds(0, 2)],
+                gat.at[p, pl.ds(0, 2)],
+                gat.at[p, pl.ds(0, 2)],
+                gat.at[p, pl.ds(0, 1)],
+            )[n]
+        else:
+            ref = (gat.at[p, pl.ds(0, NZ - 1), 0], gat.at[p, pl.ds(0, 4)], gat.at[p, pl.ds(0, 2)])[n]
         return stage(p, n, ref, there(1, 0))
+
+    def by_rows(p, n):
+        if n > 0:
+            with jax.named_scope("r%d_%d" % (n, p)):
+                stage_all(p, n - 1).wait_recv()
+        if n == 0:
+            for dx in (1, -1):
+                stage(p, 0, gat.at[p, z, x], there(0, dx)).start()
+        elif n == 1:
+            dx = 1 if p % 4 == 1 else -1
+            stage(p, 1, gat.at[p, z, column_of(-dx)], there(0, dx)).start()
+        elif n < 5:
+            for dz in (1, -1):
+                row = lax.rem(z - dz * (n - 2) + NZ, NZ)
+                stage(p, n, gat.at[p, row], there(dz, 0)).start()
+        else:
+            for dz, part in ((1, 0), (-1, NX // 2)):
+                row = lax.rem(z - dz * 3 + NZ, NZ)
+                stage(p, n, gat.at[p, row, pl.ds(part, NX // 2)], there(dz, 0)).start()
 
     def column_of(dx):
         return lax.rem(x + dx + NX, NX)
 
     def along_z(p):
-        for dz in range(1, NZ):
+        for dz in (4, 3, 5, 2, 6, 1, 7):
             stage(p, 0, gat.at[p, z, x], there(dz, 0)).start()
 
     def along_x(p):
@@ -115,12 +151,19 @@
 
     def arrived(p):
         with jax.named_scope("x3_%d" % p):
-            stage_all(p, 2).wait_recv()
-
+            stage_all(p, 5 if p in ROW_FIRST else 2).wait_recv()
+
+    along_z(0)
     weights_start(0)
-    for p in range(pairs):
+    for p in ROW_FIRST:
+        by_rows(p, 0)
+    for p in range(1, 4):
         along_z(p)
+    for p in ROW_FIRST:
+        by_rows(p, 1)
     along_x(0)
+    for p in ROW_FIRST:
+        by_rows(p, 2)
     with jax.named_scope("w0"):
         weights_all(0).wait_recv()
     weights_start(1)
@@ -168,8 +211,8 @@
     for p in range(pairs):
         with jax.named_scope("kv"):
             lax.fori_loop(p, p + 1 + nothing, keys_values, 0)
-        for move, n in moves[p]:
-            move(n)
+        for move, *n in moves[p]:
+            move(*n)
 
     with jax.named_scope("w1"):
         weights_all(1).wait_recv()
@@ -182,6 +225,9 @@
 
     def project_queries(p):
         arrived(p)
+        queries_of(p)
+
+    def queries_of(p):
         both = gat[p].reshape(tests, 2 * width).T
         for u in range(2):
             th, tl = split(both[u * width : (u + 1) * width])
@@ -358,10 +404,12 @@
             if s == (6 if g in Z_FIRST else 3):
                 finish(g)
 
-    def att(first, last):
+    def att(first, last, ahead):
         group = max(g for g in range(len(GROUPS)) if starts[g] <= first)
 
         def body(f, c):
+            if ahead is not None:
+                queries_of(ahead)
             attend(starts[group], GROUPS[group], f)
             return c
 
@@ -369,32 +417,36 @@
             lax.fori_loop(first, last + nothing, body, 0)
 
     schedule = [
-        (0, 1, [(project_queries, 0)], []),
-        (1, 3, [(further_x, 2), (along_x, 4), (project_queries, 1)], [(0, 0)]),
-        (3, 5, [(further_x, 3), (along_x, 5), (project_queries, 2)], [(0, 1)]),
-        (5, 6, [(further_x, 4), (project_queries, 3)], [(1, 0)]),
-        (6, 7, [(further_x, 5)], [(0, 2)]),
-        (7, 8, [(project_queries, 4)], [(2, 0), (1, 1)]),
-        (8, 9, [], [(0, 3)]),
-        (9, 10, [(project_queries, 5)], [(3, 0), (2, 1)]),
-        (10, 11, [], [(4, 0), (1, 2), (0, 4)]),
-        (11, 12, [],
-         [(5, 0), (2, 2), (3, 1), (0, 5), (4, 1), (5, 1), (2, 3), (0, 6), (3, 2), (4, 2), (1, 3)]
-         + [(2, 4), (5, 2), (2, 5), (3, 3), (4, 3), (2, 6), (5, 3)]),
+        (0, 1, None, [(project_queries, 0), (by_rows, 4, 3), (by_rows, 5, 3)], []),
+        (1, 3, None, [(further_x, 2), (project_queries, 1)], [(0, 0)]),
+        (3, 4, 2, [(further_x, 3), (by_rows, 4, 4), (by_rows, 5, 4), (arrived, 2)], []),
+        (4, 5, None, [], [(0, 1), (by_rows, 4, 5)]),
+        (5, 6, 3, [(arrived, 3)], [(1, 0), (by_rows, 5, 5)]),
+        (6, 7, None, [], [(0, 2)]),
+        (7, 8, 4, [(arrived, 4)], [(2, 0), (1, 1)]),
+        (8, 9, None, [], [(0, 3)]),
+        (9, 10, 5, [(arrived, 5)], [(3, 0)]),
+        (10, 11, None, [], [(4, 0), (2, 1), (0, 4)]),
+        (11, 12, None, [],
+         [(5, 0), (1, 2), (3, 1), (4, 1), (0, 5), (2, 2), (5, 1), (3, 2), (1, 3), (4, 2)]
+         + [(0, 6), (5, 2), (2, 3), (3, 3), (4, 3), (5, 3)]),
     ]
-    for first, last, before, ticks in schedule:
-        for act, n in before:
-            act(n)
+    for first, last, ahead, before, ticks in schedule:
+        for act, *n in before:
+            act(*n)
         if first == 0:
             scores(0, 0)
-        att(first, last)
-        for g, s in ticks:
-            tick(g, s)
+        att(first, last, ahead)
+        for act in ticks:
+            if len(act) == 2:
+                tick(*act)
+            else:
+                act[0](*act[1:])
 
     for half in range(2):
         weights_all(half).wait_send()
     for p in range(pairs):
-        for n in range(3):
+        for n in range(6 if p in ROW_FIRST else 3):
             stage_all(p, n).wait_send()
     for g in range(len(GROUPS)):
         sent = [own[g].at[pl.ds(0, 7)], own[g].at[0, pl.ds(0, 3)]]
@@ -419,9 +471,9 @@
     dma = pltpu.SemaphoreType.DMA
     out = pl.pallas_call(
         kernel,
-        out_shape=jax.ShapeDtypeStruct((features, mine, width), F32),
-        in_specs=[pl.BlockSpec(memory_space=pl.ANY)] + [vmem] * 5,
-        out_specs=vmem,
+        out_shape=pltpu.VMEM((features, mine, width), F32),
+        in_specs=[pl.BlockSpec(memory_space=pl.ANY)] * 6,
+        out_specs=pl.BlockSpec(memory_space=pltpu.VMEM),
         scratch_shapes=[
             pltpu.VMEM((features, width, rows), F32),
             pltpu.VMEM((2, NF, width // NF, 2 * width), F32),
@@ -438,12 +490,15 @@
             dma((features,)),
             dma((2,)),
             dma((2,)),
-            dma((features // 2, 3)),
-            dma((features // 2, 3)),
+            dma((features // 2, 6)),
+            dma((features // 2, 6)),
             dma((len(GROUPS),)),
             dma((len(GROUPS), 10)),
             [pltpu.VMEM((NZ, NX, mine, lanes(n)), F32) for n in GROUPS],
             inboxes,
+            pltpu.VMEM((features, mine, width), F32),
+            pltpu.VMEM((4, width // NF, width), F32),
+            dma((5,)),
         ],
         compiler_params=pltpu.CompilerParams(
             collective_id=0, has_side_effects=True, vmem_limit_bytes=60 * 2**20

time: 69.7 us -> 65 us (0.933)
  Pallas kernels: 67.5 us -> 63.6 us
  local copies, waits for them, and re-layouts: 1.54 us -> 0.64 us
    pallas_call x1, Pallas kernels: 67.5 us -> 63.6 us  [per_device(): pl.pallas_call(kernel, out_shape=pltpu.VMEM((features, mine, width), F32)...]
    unnamed x1, local copies, waits for them, and re-layouts: 1.54 us -> 0.64 us
where the time goes in v4:
time: 65 us; the launch traced here: 64.3 us
  Pallas kernels  63.6 us (98%)
    pallas_call x1, Pallas kernels, per_device(): pl.pallas_call(kernel, out_shape=pltpu.VMEM((features, mine, width), F32)...  63.6 us

profile of v4, /device:TPU:2, one launch (start us, length us, event | category | flops | bytes accessed | tf_op | source)
XLA Modules:
  0.0 64.3 jit_solution(1423365580969835019)
XLA Ops:
  0.0 63.6 %attention.1 = f32[12,8,192]{2,1,0:T(8,128)S(1)} custom-call(f32[12,192,512]{2,1,0:T(8,128)} %bitcast.4, f32[12,8,192]{2,1,0:T(8,128)} %bitcast.5, f32[24,192]{1,0:T(8,128)} %wq_hbm.1, f32[24,192]{1,0:T(8,128)} %wk_hbm.1, f32[24,192]{1,0:T(8,128)} %wv_hbm.1, f32[24,192]{1,0:T(8,128)} %wo_hbm.1), custom_call_target="tpu_custom_call" | custom-call | tf_op jit(solution)/shard_map/attention/pallas_call | solution.py:472
  63.6 0.6 %copy.8 = f32[8,12,192]{2,0,1:T(8,128)} copy(f32[8,12,192]{2,0,1:T(8,128)S(1)} %bitcast.3) | data formatting | bytes 147456

commit v5 on v4

--- a/solution.py
+++ b/solution.py
@@ -204,7 +204,7 @@
         [(along_x, 1)],
         [],
         [(further_x, 0), (along_x, 2)],
-        [],
+        [(by_rows, 4, 3), (by_rows, 5, 3)],
         [],
         [(further_x, 1), (along_x, 3)],
     ]
@@ -417,19 +417,20 @@
             lax.fori_loop(first, last + nothing, body, 0)
 
     schedule = [
-        (0, 1, None, [(project_queries, 0), (by_rows, 4, 3), (by_rows, 5, 3)], []),
-        (1, 3, None, [(further_x, 2), (project_queries, 1)], [(0, 0)]),
-        (3, 4, 2, [(further_x, 3), (by_rows, 4, 4), (by_rows, 5, 4), (arrived, 2)], []),
-        (4, 5, None, [], [(0, 1), (by_rows, 4, 5)]),
-        (5, 6, 3, [(arrived, 3)], [(1, 0), (by_rows, 5, 5)]),
-        (6, 7, None, [], [(0, 2)]),
-        (7, 8, 4, [(arrived, 4)], [(2, 0), (1, 1)]),
-        (8, 9, None, [], [(0, 3)]),
-        (9, 10, 5, [(arrived, 5)], [(3, 0)]),
-        (10, 11, None, [], [(4, 0), (2, 1), (0, 4)]),
+        (0, 1, None, [(project_queries, 0)], []),
+        (1, 3, None, [(further_x, 2), (by_rows, 4, 4), (by_rows, 5, 4), (project_queries, 1)],
+         [(0, 0), (by_rows, 4, 5), (by_rows, 5, 5)]),
+        (3, 4, 2, [(further_x, 3), (arrived, 2)], []),
+        (4, 5, None, [], []),
+        (5, 6, 3, [(arrived, 3)], [(1, 0), (0, 1)]),
+        (6, 7, None, [], []),
+        (7, 8, 4, [(arrived, 4)], [(2, 0), (1, 1), (0, 2)]),
+        (8, 9, None, [], []),
+        (9, 10, 5, [(arrived, 5)], [(3, 0), (2, 1)]),
+        (10, 11, None, [], [(4, 0), (0, 3)]),
         (11, 12, None, [],
-         [(5, 0), (1, 2), (3, 1), (4, 1), (0, 5), (2, 2), (5, 1), (3, 2), (1, 3), (4, 2)]
-         + [(0, 6), (5, 2), (2, 3), (3, 3), (4, 3), (5, 3)]),
+         [(5, 0), (1, 2), (3, 1), (2, 2), (4, 1), (5, 1), (0, 4), (3, 2), (4, 2), (5, 2)]
+         + [(1, 3), (0, 5), (2, 3), (0, 6), (3, 3), (4, 3), (5, 3)]),
     ]
     for first, last, ahead, before, ticks in schedule:
         for act, *n in before:

time: 65 us -> 64.3 us (0.989)
  no operation moved by 1% of the time
where the time goes in v5:
time: 64.3 us; the launch traced here: 64.1 us
  Pallas kernels  63.5 us (99%)
    pallas_call x1, Pallas kernels, per_device(): pl.pallas_call(kernel, out_shape=pltpu.VMEM((features, mine, width), F32)...  63.5 us

profile of v5, /device:TPU:2, one launch (start us, length us, event | category | flops | bytes accessed | tf_op | source)
XLA Modules:
  0.0 64.1 jit_solution(9693019304125407259)
XLA Ops:
  0.0 63.5 %attention.1 = f32[12,8,192]{2,1,0:T(8,128)S(1)} custom-call(f32[12,192,512]{2,1,0:T(8,128)} %bitcast.4, f32[12,8,192]{2,1,0:T(8,128)} %bitcast.5, f32[24,192]{1,0:T(8,128)} %wq_hbm.1, f32[24,192]{1,0:T(8,128)} %wk_hbm.1, f32[24,192]{1,0:T(8,128)} %wv_hbm.1, f32[24,192]{1,0:T(8,128)} %wo_hbm.1), custom_call_target="tpu_custom_call" | custom-call | tf_op jit(solution)/shard_map/attention/pallas_call | solution.py:473
  63.5 0.6 %copy.8 = f32[8,12,192]{2,0,1:T(8,128)} copy(f32[8,12,192]{2,0,1:T(8,128)S(1)} %bitcast.3) | data formatting | bytes 147456
